TPU v7x, 32 devices: a whole 2x2x4 slice. The times are simulated.
32 devices in a mesh: seq: 8 (over y, x, core), head: 4 (over z).
Axes of the slice: x: 2, y: 2, z: 4, core: 2. Of those that a mesh axis runs over, the one named last changes fastest.
Arguments:
- text_states: bfloat16 [2048, 4096], P('seq', 'head'), may hold values from -200 to 200
- query_weight: bfloat16 [4096, 4096], P(None, 'head'), may hold values from -0.09375 to 0.09375
- image_keys: bfloat16 [4096, 1024], P('seq', 'head'), may hold values from -12 to 12
- image_values: bfloat16 [4096, 1024], P('seq', 'head'), may hold values from -24 to 24
- output_weight: bfloat16 [4096, 4096], P('head'), may hold values from -0.09375 to 0.09375
- attn_gate: float32 [1], replicated, may hold values from 0.3 to 1.5
- frame_lengths: int32 [16], replicated, may hold values from 1 to 512, 4096 in all
- frame_limit: int32 [32], replicated, may hold values from 0 to 16
Outputs:
- gated_branch: bfloat16 [2048, 4096], P('seq', 'head')
Inputs may be any that keep to these rules, and one draw needn't show every extreme that they name: `frame_lengths`: the lengths sum to 4096.
All inputs are finite; a program needn't handle non-finite values.
Results may differ from a plain program's by a relative error of at most 0.014.
The roundings to bfloat16 on the way count: a program that leaves them out, or rounds other values in their place, can miss the bound.
Values may be sent and summed in bfloat16 or wider, within the bound.
No kernel may reach another device: no remote copies, remote signals or barrier semaphores. Data moves between devices by JAX's collectives and lax.ppermute only.
A program may use at most 128 MiB of HBM per device.

v0:
```python
import math
import jax
import jax.numpy as jnp
from jax import lax
from jax.sharding import PartitionSpec as P

HD = 128
TBLK = 64
GROUP = 4
masked_fill = -1e30


def from_behind(block, axis, distance):
    devices = range(lax.axis_size(axis))
    route = [((i - distance) % len(devices), i) for i in devices]
    return lax.ppermute(block, axis, route)


def shards(
    text_states,
    query_weight,
    image_keys,
    image_values,
    output_weight,
    attn_gate,
    frame_lengths,
    frame_limit,
):
    text_rows = text_states.shape[0]
    video_rows = image_keys.shape[0]
    local_kv = image_keys.shape[1] // HD
    seq_index = lax.axis_index("seq")
    cycle_size = lax.axis_size("seq")
    score_scale = 1.0 / math.sqrt(HD)
    queries = jnp.dot(
        lax.all_gather(text_states, "head", axis=1, tiled=True),
        query_weight,
        preferred_element_type=jnp.float32,
    ).astype(jnp.bfloat16)
    grouped_queries = (
        queries.reshape(text_rows, local_kv, GROUP, HD)
        .transpose(1, 2, 0, 3)
        .reshape(local_kv, GROUP * text_rows, HD)
    )
    frame_ends = jnp.cumsum(frame_lengths)
    block_count = text_rows // TBLK
    my_limits = lax.dynamic_slice_in_dim(frame_limit, seq_index * block_count, block_count, 0)
    group_limits = jnp.tile(jnp.repeat(my_limits, TBLK), GROUP)

    def dense_block(running, key_block, value_block, key_frames):
        best_score, weight_sum, accumulated = running
        key_head_count = key_block.reshape(key_block.shape[0], local_kv, HD)
        value_heads = value_block.reshape(value_block.shape[0], local_kv, HD)
        scores = (
            jnp.einsum(
                "sxn,lsn->sxl", grouped_queries, key_head_count, preferred_element_type=jnp.float32
            )
            * score_scale
        )
        visible = key_frames[None, None, :] < group_limits[None, :, None]
        block_best = jnp.max(jnp.where(visible, scores, masked_fill), axis=2)
        new_best = jnp.maximum(best_score, block_best)
        weights = jnp.where(visible, jnp.exp(scores - new_best[:, :, None]), 0.0)
        factor = jnp.exp(best_score - new_best)
        weight_sum = weight_sum * factor + jnp.sum(weights, axis=2)
        mixed = jnp.einsum(
            "vus,svg->vug",
            weights.astype(jnp.bfloat16),
            value_heads,
            preferred_element_type=jnp.float32,
        )
        accumulated = accumulated * factor[:, :, None] + mixed
        return (new_best, weight_sum, accumulated)

    def attend_frames(running, key_block, value_block, first_row):
        token_positions = first_row + jnp.arange(key_block.shape[0], dtype=jnp.int32)
        key_frames = jnp.sum(
            (frame_ends[None, :] <= token_positions[:, None]).astype(jnp.int32), axis=1
        )
        return dense_block(running, key_block, value_block, key_frames)

    initial = (
        jnp.full((local_kv, GROUP * text_rows), masked_fill, jnp.float32),
        jnp.zeros((local_kv, GROUP * text_rows), jnp.float32),
        jnp.zeros((local_kv, GROUP * text_rows, HD), jnp.float32),
    )
    half_rows = video_rows // 2

    def paired_turn(turn_index, state_in):
        running, keys_up, values_up, keys_down, values_down = state_in
        source_up = (seq_index - turn_index) % cycle_size
        source_down = (seq_index + turn_index) % cycle_size
        running = attend_frames(running, keys_up, values_up, source_up * video_rows)
        running = attend_frames(
            running, keys_down, values_down, source_down * video_rows + half_rows
        )
        keys_up, values_up = from_behind((keys_up, values_up), "seq", 1)
        keys_down, values_down = from_behind((keys_down, values_down), "seq", -1)
        return (running, keys_up, values_up, keys_down, values_down)

    start_state = (
        initial,
        image_keys[:half_rows],
        image_values[:half_rows],
        image_keys[half_rows:],
        image_values[half_rows:],
    )
    running, keys_up, values_up, keys_down, values_down = lax.fori_loop(
        0, cycle_size - 1, paired_turn, start_state
    )
    running = attend_frames(running, keys_up, values_up, (seq_index + 1) % cycle_size * video_rows)
    running = attend_frames(
        running, keys_down, values_down, (seq_index - 1) % cycle_size * video_rows + half_rows
    )
    best_score, weight_sum, accumulated = running
    output_groups = (accumulated / jnp.maximum(weight_sum, 1.0)[:, :, None]).astype(jnp.bfloat16)
    attention_output = (
        output_groups.reshape(local_kv, GROUP, text_rows, HD)
        .transpose(2, 0, 1, 3)
        .reshape(text_rows, local_kv * GROUP * HD)
    )
    summed = lax.psum_scatter(
        lax.dot_general(
            output_weight,
            attention_output,
            (((0,), (1,)), ((), ())),
            preferred_element_type=jnp.float32,
        ).astype(jnp.bfloat16),
        "head",
        scatter_dimension=0,
        tiled=True,
    ).astype(jnp.float32)
    return (jnp.tanh(attn_gate[0]) * summed.T).astype(jnp.bfloat16)


def solution(mesh):
    in_specs = (
        P("seq", "head"),
        P(None, "head"),
        P("seq", "head"),
        P("seq", "head"),
        P("head", None),
        P(),
        P(),
        P(),
    )
    out_specs = P("seq", "head")
    return jax.shard_map(shards, mesh=mesh, in_specs=in_specs, out_specs=out_specs, check_vma=False)
```

profile of v0, /device:TPU:0, one launch (start us, length us, event | category | flops | bytes accessed | tf_op | source)
XLA Modules:
  0.0 186.2 jit_solution(13264895358251018407)
XLA Ops:
  6.5 0.7 all-gather.2.cloned.1.call-update
  7.4 0.7 copy.44
  8.3 0.7 dynamic_slice.3
  9.6 1.1 fusion.71
  10.8 46.5 %all-gather.2.cloned.1.call-done = bf16[256,4096]{1,0:T(8,128)(2,1)} async-done(((bf16[256,1024]{1,0:T(8,128)(2,1)}), bf16[256,4096]{1,0:T(8,128)(2,1)}) %all-gather.2.cloned.1.call-update) | async-done | bytes 2097168 | tf_op jit(solution)/shard_map/all_gather | solution.py:36
  57.3 6.3 %convolution_convert_fusion.1 = bf16[256,1024]{1,0:T(8,128)(2,1)S(1)} fusion(bf16[256,4096]{1,0:T(8,128)(2,1)} %all-gather.2.cloned.1.call-done, bf16[4096,1024]{1,0:T(8,128)(2,1)} %param.11), kind=kOutput, calls=%fused_computation.65 | convolution fusion | flops 2147745792 | bytes 11010048 | tf_op jit(solution)/shard_map/dot_general | solution.py:35
  64.1 59.5 %while.28 = (s32[]{:T(128)}, f32[2,1024]{1,0:T(2,128)S(1)}, f32[2,1024]{1,0:T(2,128)S(1)}, f32[2,1024,128]{2,1,0:T(8,128)S(1)}, bf16[256,256]{1,0:T(8,128)(2,1)S...) while((s32[]{:T(128)}, f32[2,1024]{1,0:T(2,128)S(1)}, ...), condition=%wide.region_8.9_spmd.clone, body=%wide.region_1.8_spmd.clone.sunk | while | flops 550279168 | bytes 23832240 | solution.py:108
  64.4 1.6 collective-permute-start.1
  66.0 1.1 collective-permute-start.2
  67.2 0.5 collective-permute-start.3
  68.2 0.6 select_reduce_fusion.6
  68.8 0.6 select_reduce_fusion.7
  69.4 0.5 fusion.116
  69.9 0.5 fusion.115
  70.4 1.2 fusion.118
  71.7 0.8 convolution_add_fusion.5
  72.6 1.2 collective-permute-start
  73.9 2.7 %collective-permute-start.2 = (bf16[256,256]{1,0:T(8,128)(2,1)S(1)}, bf16[256,256]{1,0:T(8,128)(2,1)S(1)}, u32[]{:S(2)}, u32[]{:S(2)}) collective-permute-start(bf16[256,256]{1,0:T(8,128)(2,1)S(1)} %copy.131), channel_id=1, source_target_pairs={{4,0},{8,4},{12,8},{16,12},{20,16},{24,20},{28,24},{0,28},{5,1},{9... | collective-permute-start | bytes 393224 | tf_op jit(solution)/shard_map/while/body/eval_jaxpr/ppermute | solution.py:16
  77.2 0.6 select_reduce_fusion.6
  77.7 0.6 select_reduce_fusion.7
  78.3 0.5 fusion.116
  79.4 1.2 fusion.118
  80.6 0.8 convolution_add_fusion.5
  81.5 0.8 collective-permute-start
  82.5 2.7 %collective-permute-start.2 = (bf16[256,256]{1,0:T(8,128)(2,1)S(1)}, bf16[256,256]{1,0:T(8,128)(2,1)S(1)}, u32[]{:S(2)}, u32[]{:S(2)}) collective-permute-start(bf16[256,256]{1,0:T(8,128)(2,1)S(1)} %copy.131), channel_id=1, source_target_pairs={{4,0},{8,4},{12,8},{16,12},{20,16},{24,20},{28,24},{0,28},{5,1},{9... | collective-permute-start | bytes 393224 | tf_op jit(solution)/shard_map/while/body/eval_jaxpr/ppermute | solution.py:16
  85.8 0.6 select_reduce_fusion.6
  86.3 0.6 select_reduce_fusion.7
  86.9 0.5 fusion.116
  88.0 1.2 fusion.118
  89.2 0.8 convolution_add_fusion.5
  90.7 2.7 %collective-permute-start.2 = (bf16[256,256]{1,0:T(8,128)(2,1)S(1)}, bf16[256,256]{1,0:T(8,128)(2,1)S(1)}, u32[]{:S(2)}, u32[]{:S(2)}) collective-permute-start(bf16[256,256]{1,0:T(8,128)(2,1)S(1)} %copy.131), channel_id=1, source_target_pairs={{4,0},{8,4},{12,8},{16,12},{20,16},{24,20},{28,24},{0,28},{5,1},{9... | collective-permute-start | bytes 393224 | tf_op jit(solution)/shard_map/while/body/eval_jaxpr/ppermute | solution.py:16
  94.0 0.6 select_reduce_fusion.6
  94.6 0.6 select_reduce_fusion.7
  95.2 0.5 fusion.116
  96.2 1.2 fusion.118
  97.5 0.8 convolution_add_fusion.5
  99.0 2.7 %collective-permute-start.2 = (bf16[256,256]{1,0:T(8,128)(2,1)S(1)}, bf16[256,256]{1,0:T(8,128)(2,1)S(1)}, u32[]{:S(2)}, u32[]{:S(2)}) collective-permute-start(bf16[256,256]{1,0:T(8,128)(2,1)S(1)} %copy.131), channel_id=1, source_target_pairs={{4,0},{8,4},{12,8},{16,12},{20,16},{24,20},{28,24},{0,28},{5,1},{9... | collective-permute-start | bytes 393224 | tf_op jit(solution)/shard_map/while/body/eval_jaxpr/ppermute | solution.py:16
  102.3 0.6 select_reduce_fusion.6
  102.8 0.6 select_reduce_fusion.7
  103.4 0.5 fusion.116
  104.5 1.2 fusion.118
  105.7 0.8 convolution_add_fusion.5
  106.6 0.7 collective-permute-start
  107.4 2.7 %collective-permute-start.2 = (bf16[256,256]{1,0:T(8,128)(2,1)S(1)}, bf16[256,256]{1,0:T(8,128)(2,1)S(1)}, u32[]{:S(2)}, u32[]{:S(2)}) collective-permute-start(bf16[256,256]{1,0:T(8,128)(2,1)S(1)} %copy.131), channel_id=1, source_target_pairs={{4,0},{8,4},{12,8},{16,12},{20,16},{24,20},{28,24},{0,28},{5,1},{9... | collective-permute-start | bytes 393224 | tf_op jit(solution)/shard_map/while/body/eval_jaxpr/ppermute | solution.py:16
  110.7 0.6 select_reduce_fusion.6
  111.3 0.6 select_reduce_fusion.7
  111.9 0.5 fusion.116
  112.9 1.2 fusion.118
  114.2 0.8 convolution_add_fusion.5
  115.1 0.8 collective-permute-start
  116.0 2.7 %collective-permute-start.2 = (bf16[256,256]{1,0:T(8,128)(2,1)S(1)}, bf16[256,256]{1,0:T(8,128)(2,1)S(1)}, u32[]{:S(2)}, u32[]{:S(2)}) collective-permute-start(bf16[256,256]{1,0:T(8,128)(2,1)S(1)} %copy.131), channel_id=1, source_target_pairs={{4,0},{8,4},{12,8},{16,12},{20,16},{24,20},{28,24},{0,28},{5,1},{9... | collective-permute-start | bytes 393224 | tf_op jit(solution)/shard_map/while/body/eval_jaxpr/ppermute | solution.py:16
  119.3 0.6 select_reduce_fusion.6
  119.8 0.6 select_reduce_fusion.7
  120.4 0.5 fusion.116
  121.5 1.2 fusion.118
  122.7 0.8 convolution_add_fusion.5
  123.6 0.6 select_reduce_fusion.2
  124.2 0.6 select_reduce_fusion.3
  124.8 0.5 fusion.36
  125.8 1.2 fusion.41
  127.1 1.0 fusion.42
  128.3 7.1 %fusion.35 = bf16[4096,256]{0,1:T(8,128)(2,1)} fusion(bf16[256,1024]{0,1:T(8,128)(2,1)S(1)} %bitcast.115, bf16[1024,4096]{1,0:T(8,128)(2,1)} %param.14), kind=kOutput, calls=%fused_computation.51 | convolution fusion | flops 2148532224 | bytes 11010048 | tf_op jit(solution)/shard_map/dot_general | solution.py:123
  136.1 41.3 %reduce-scatter.2.cloned.1.call-done = bf16[1024,256]{0,1:T(8,128)(2,1)} async-done(((bf16[4096,256]{0,1:T(8,128)(2,1)}), bf16[1024,256]{0,1:T(8,128)(2,1)}) %reduce-scatter.2.cloned.1.call-update) | async-done | bytes 524304 | tf_op jit(solution)/shard_map/reduce_scatter | solution.py:122
  177.4 1.9 %fusion.53 = bf16[256,1024]{1,0:T(8,128)(2,1)} fusion(bf16[1024,256]{0,1:T(8,128)(2,1)} %reduce-scatter.2.cloned.1.call-done, f32[]{:T(128)} %bitcast), kind=kLoop, calls=%fused_computation.75 | loop fusion | flops 786432 | bytes 1048580 | tf_op jit(solution)/shard_map/convert_element_type | solution.py:133
  (154 shorter events, 11.0 us)
Async XLA Ops:
  6.5 50.8 %all-gather.2.cloned.1.call-start = ((), (), s32[]{:S(2)}) async-start(), calls=%async_computation.1 | async-start | bytes 2621440 | tf_op jit(solution)/shard_map/all_gather | solution.py:36
  7.3 170.1 %reduce-scatter.2.cloned.1.call-start = ((), (), s32[]{:S(2)}) async-start(), calls=%async_computation.2 | async-start | bytes 2621440 | tf_op jit(solution)/shard_map/reduce_scatter | solution.py:122
  64.3 8.2 %collective-permute-start = (bf16[256,256]{1,0:T(8,128)(2,1)S(1)}, bf16[256,256]{1,0:T(8,128)(2,1)S(1)}, u32[]{:S(2)}, u32[]{:S(2)}) collective-permute-start(bf16[256,256]{1,0:T(8,128)(2,1)S(1)} %copy.129), channel_id=1, source_target_pairs={{28,0},{0,4},{4,8},{8,12},{12,16},{16,20},{20,24},{24,28},{29,1},{... | collective-permute-start | bytes 393224 | tf_op jit(solution)/shard_map/while/body/eval_jaxpr/ppermute | solution.py:16
  64.4 8.1 %collective-permute-start.1 = (bf16[256,256]{1,0:T(8,128)(2,1)S(1)}, bf16[256,256]{1,0:T(8,128)(2,1)S(1)}, u32[]{:S(2)}, u32[]{:S(2)}) collective-permute-start(bf16[256,256]{1,0:T(8,128)(2,1)S(1)} %copy.130), channel_id=1, source_target_pairs={{28,0},{0,4},{4,8},{8,12},{12,16},{16,20},{20,24},{24,28},{29,1},{... | collective-permute-start | bytes 393224 | tf_op jit(solution)/shard_map/while/body/eval_jaxpr/ppermute | solution.py:16
  66.0 6.5 %collective-permute-start.2 = (bf16[256,256]{1,0:T(8,128)(2,1)S(1)}, bf16[256,256]{1,0:T(8,128)(2,1)S(1)}, u32[]{:S(2)}, u32[]{:S(2)}) collective-permute-start(bf16[256,256]{1,0:T(8,128)(2,1)S(1)} %copy.131), channel_id=1, source_target_pairs={{4,0},{8,4},{12,8},{16,12},{20,16},{24,20},{28,24},{0,28},{5,1},{9... | collective-permute-start | bytes 393224 | tf_op jit(solution)/shard_map/while/body/eval_jaxpr/ppermute | solution.py:16
  67.2 5.3 %collective-permute-start.3 = (bf16[256,256]{1,0:T(8,128)(2,1)S(1)}, bf16[256,256]{1,0:T(8,128)(2,1)S(1)}, u32[]{:S(2)}, u32[]{:S(2)}) collective-permute-start(bf16[256,256]{1,0:T(8,128)(2,1)S(1)} %copy.132), channel_id=1, source_target_pairs={{4,0},{8,4},{12,8},{16,12},{20,16},{24,20},{28,24},{0,28},{5,1},{9... | collective-permute-start | bytes 393224 | tf_op jit(solution)/shard_map/while/body/eval_jaxpr/ppermute | solution.py:16
  72.6 8.9 %collective-permute-start = (bf16[256,256]{1,0:T(8,128)(2,1)S(1)}, bf16[256,256]{1,0:T(8,128)(2,1)S(1)}, u32[]{:S(2)}, u32[]{:S(2)}) collective-permute-start(bf16[256,256]{1,0:T(8,128)(2,1)S(1)} %copy.129), channel_id=1, source_target_pairs={{28,0},{0,4},{4,8},{8,12},{12,16},{16,20},{20,24},{24,28},{29,1},{... | collective-permute-start | bytes 393224 | tf_op jit(solution)/shard_map/while/body/eval_jaxpr/ppermute | solution.py:16
  73.8 7.7 %collective-permute-start.1 = (bf16[256,256]{1,0:T(8,128)(2,1)S(1)}, bf16[256,256]{1,0:T(8,128)(2,1)S(1)}, u32[]{:S(2)}, u32[]{:S(2)}) collective-permute-start(bf16[256,256]{1,0:T(8,128)(2,1)S(1)} %copy.130), channel_id=1, source_target_pairs={{28,0},{0,4},{4,8},{8,12},{12,16},{16,20},{20,24},{24,28},{29,1},{... | collective-permute-start | bytes 393224 | tf_op jit(solution)/shard_map/while/body/eval_jaxpr/ppermute | solution.py:16
  73.9 7.6 %collective-permute-start.2 = (bf16[256,256]{1,0:T(8,128)(2,1)S(1)}, bf16[256,256]{1,0:T(8,128)(2,1)S(1)}, u32[]{:S(2)}, u32[]{:S(2)}) collective-permute-start(bf16[256,256]{1,0:T(8,128)(2,1)S(1)} %copy.131), channel_id=1, source_target_pairs={{4,0},{8,4},{12,8},{16,12},{20,16},{24,20},{28,24},{0,28},{5,1},{9... | collective-permute-start | bytes 393224 | tf_op jit(solution)/shard_map/while/body/eval_jaxpr/ppermute | solution.py:16
  76.6 4.9 %collective-permute-start.3 = (bf16[256,256]{1,0:T(8,128)(2,1)S(1)}, bf16[256,256]{1,0:T(8,128)(2,1)S(1)}, u32[]{:S(2)}, u32[]{:S(2)}) collective-permute-start(bf16[256,256]{1,0:T(8,128)(2,1)S(1)} %copy.132), channel_id=1, source_target_pairs={{4,0},{8,4},{12,8},{16,12},{20,16},{24,20},{28,24},{0,28},{5,1},{9... | collective-permute-start | bytes 393224 | tf_op jit(solution)/shard_map/while/body/eval_jaxpr/ppermute | solution.py:16
  81.5 8.5 %collective-permute-start = (bf16[256,256]{1,0:T(8,128)(2,1)S(1)}, bf16[256,256]{1,0:T(8,128)(2,1)S(1)}, u32[]{:S(2)}, u32[]{:S(2)}) collective-permute-start(bf16[256,256]{1,0:T(8,128)(2,1)S(1)} %copy.129), channel_id=1, source_target_pairs={{28,0},{0,4},{4,8},{8,12},{12,16},{16,20},{20,24},{24,28},{29,1},{... | collective-permute-start | bytes 393224 | tf_op jit(solution)/shard_map/while/body/eval_jaxpr/ppermute | solution.py:16
  82.4 7.7 %collective-permute-start.1 = (bf16[256,256]{1,0:T(8,128)(2,1)S(1)}, bf16[256,256]{1,0:T(8,128)(2,1)S(1)}, u32[]{:S(2)}, u32[]{:S(2)}) collective-permute-start(bf16[256,256]{1,0:T(8,128)(2,1)S(1)} %copy.130), channel_id=1, source_target_pairs={{28,0},{0,4},{4,8},{8,12},{12,16},{16,20},{20,24},{24,28},{29,1},{... | collective-permute-start | bytes 393224 | tf_op jit(solution)/shard_map/while/body/eval_jaxpr/ppermute | solution.py:16
  82.5 7.6 %collective-permute-start.2 = (bf16[256,256]{1,0:T(8,128)(2,1)S(1)}, bf16[256,256]{1,0:T(8,128)(2,1)S(1)}, u32[]{:S(2)}, u32[]{:S(2)}) collective-permute-start(bf16[256,256]{1,0:T(8,128)(2,1)S(1)} %copy.131), channel_id=1, source_target_pairs={{4,0},{8,4},{12,8},{16,12},{20,16},{24,20},{28,24},{0,28},{5,1},{9... | collective-permute-start | bytes 393224 | tf_op jit(solution)/shard_map/while/body/eval_jaxpr/ppermute | solution.py:16
  85.1 4.9 %collective-permute-start.3 = (bf16[256,256]{1,0:T(8,128)(2,1)S(1)}, bf16[256,256]{1,0:T(8,128)(2,1)S(1)}, u32[]{:S(2)}, u32[]{:S(2)}) collective-permute-start(bf16[256,256]{1,0:T(8,128)(2,1)S(1)} %copy.132), channel_id=1, source_target_pairs={{4,0},{8,4},{12,8},{16,12},{20,16},{24,20},{28,24},{0,28},{5,1},{9... | collective-permute-start | bytes 393224 | tf_op jit(solution)/shard_map/while/body/eval_jaxpr/ppermute | solution.py:16
  90.1 8.2 %collective-permute-start = (bf16[256,256]{1,0:T(8,128)(2,1)S(1)}, bf16[256,256]{1,0:T(8,128)(2,1)S(1)}, u32[]{:S(2)}, u32[]{:S(2)}) collective-permute-start(bf16[256,256]{1,0:T(8,128)(2,1)S(1)} %copy.129), channel_id=1, source_target_pairs={{28,0},{0,4},{4,8},{8,12},{12,16},{16,20},{20,24},{24,28},{29,1},{... | collective-permute-start | bytes 393224 | tf_op jit(solution)/shard_map/while/body/eval_jaxpr/ppermute | solution.py:16
  90.6 7.7 %collective-permute-start.1 = (bf16[256,256]{1,0:T(8,128)(2,1)S(1)}, bf16[256,256]{1,0:T(8,128)(2,1)S(1)}, u32[]{:S(2)}, u32[]{:S(2)}) collective-permute-start(bf16[256,256]{1,0:T(8,128)(2,1)S(1)} %copy.130), channel_id=1, source_target_pairs={{28,0},{0,4},{4,8},{8,12},{12,16},{16,20},{20,24},{24,28},{29,1},{... | collective-permute-start | bytes 393224 | tf_op jit(solution)/shard_map/while/body/eval_jaxpr/ppermute | solution.py:16
  90.7 7.6 %collective-permute-start.2 = (bf16[256,256]{1,0:T(8,128)(2,1)S(1)}, bf16[256,256]{1,0:T(8,128)(2,1)S(1)}, u32[]{:S(2)}, u32[]{:S(2)}) collective-permute-start(bf16[256,256]{1,0:T(8,128)(2,1)S(1)} %copy.131), channel_id=1, source_target_pairs={{4,0},{8,4},{12,8},{16,12},{20,16},{24,20},{28,24},{0,28},{5,1},{9... | collective-permute-start | bytes 393224 | tf_op jit(solution)/shard_map/while/body/eval_jaxpr/ppermute | solution.py:16
  93.4 4.9 %collective-permute-start.3 = (bf16[256,256]{1,0:T(8,128)(2,1)S(1)}, bf16[256,256]{1,0:T(8,128)(2,1)S(1)}, u32[]{:S(2)}, u32[]{:S(2)}) collective-permute-start(bf16[256,256]{1,0:T(8,128)(2,1)S(1)} %copy.132), channel_id=1, source_target_pairs={{4,0},{8,4},{12,8},{16,12},{20,16},{24,20},{28,24},{0,28},{5,1},{9... | collective-permute-start | bytes 393224 | tf_op jit(solution)/shard_map/while/body/eval_jaxpr/ppermute | solution.py:16
  98.4 8.2 %collective-permute-start = (bf16[256,256]{1,0:T(8,128)(2,1)S(1)}, bf16[256,256]{1,0:T(8,128)(2,1)S(1)}, u32[]{:S(2)}, u32[]{:S(2)}) collective-permute-start(bf16[256,256]{1,0:T(8,128)(2,1)S(1)} %copy.129), channel_id=1, source_target_pairs={{28,0},{0,4},{4,8},{8,12},{12,16},{16,20},{20,24},{24,28},{29,1},{... | collective-permute-start | bytes 393224 | tf_op jit(solution)/shard_map/while/body/eval_jaxpr/ppermute | solution.py:16
  98.9 7.7 %collective-permute-start.1 = (bf16[256,256]{1,0:T(8,128)(2,1)S(1)}, bf16[256,256]{1,0:T(8,128)(2,1)S(1)}, u32[]{:S(2)}, u32[]{:S(2)}) collective-permute-start(bf16[256,256]{1,0:T(8,128)(2,1)S(1)} %copy.130), channel_id=1, source_target_pairs={{28,0},{0,4},{4,8},{8,12},{12,16},{16,20},{20,24},{24,28},{29,1},{... | collective-permute-start | bytes 393224 | tf_op jit(solution)/shard_map/while/body/eval_jaxpr/ppermute | solution.py:16
  99.0 7.6 %collective-permute-start.2 = (bf16[256,256]{1,0:T(8,128)(2,1)S(1)}, bf16[256,256]{1,0:T(8,128)(2,1)S(1)}, u32[]{:S(2)}, u32[]{:S(2)}) collective-permute-start(bf16[256,256]{1,0:T(8,128)(2,1)S(1)} %copy.131), channel_id=1, source_target_pairs={{4,0},{8,4},{12,8},{16,12},{20,16},{24,20},{28,24},{0,28},{5,1},{9... | collective-permute-start | bytes 393224 | tf_op jit(solution)/shard_map/while/body/eval_jaxpr/ppermute | solution.py:16
  101.7 4.9 %collective-permute-start.3 = (bf16[256,256]{1,0:T(8,128)(2,1)S(1)}, bf16[256,256]{1,0:T(8,128)(2,1)S(1)}, u32[]{:S(2)}, u32[]{:S(2)}) collective-permute-start(bf16[256,256]{1,0:T(8,128)(2,1)S(1)} %copy.132), channel_id=1, source_target_pairs={{4,0},{8,4},{12,8},{16,12},{20,16},{24,20},{28,24},{0,28},{5,1},{9... | collective-permute-start | bytes 393224 | tf_op jit(solution)/shard_map/while/body/eval_jaxpr/ppermute | solution.py:16
  106.6 8.4 %collective-permute-start = (bf16[256,256]{1,0:T(8,128)(2,1)S(1)}, bf16[256,256]{1,0:T(8,128)(2,1)S(1)}, u32[]{:S(2)}, u32[]{:S(2)}) collective-permute-start(bf16[256,256]{1,0:T(8,128)(2,1)S(1)} %copy.129), channel_id=1, source_target_pairs={{28,0},{0,4},{4,8},{8,12},{12,16},{16,20},{20,24},{24,28},{29,1},{... | collective-permute-start | bytes 393224 | tf_op jit(solution)/shard_map/while/body/eval_jaxpr/ppermute | solution.py:16
  107.3 7.7 %collective-permute-start.1 = (bf16[256,256]{1,0:T(8,128)(2,1)S(1)}, bf16[256,256]{1,0:T(8,128)(2,1)S(1)}, u32[]{:S(2)}, u32[]{:S(2)}) collective-permute-start(bf16[256,256]{1,0:T(8,128)(2,1)S(1)} %copy.130), channel_id=1, source_target_pairs={{28,0},{0,4},{4,8},{8,12},{12,16},{16,20},{20,24},{24,28},{29,1},{... | collective-permute-start | bytes 393224 | tf_op jit(solution)/shard_map/while/body/eval_jaxpr/ppermute | solution.py:16
  107.4 7.6 %collective-permute-start.2 = (bf16[256,256]{1,0:T(8,128)(2,1)S(1)}, bf16[256,256]{1,0:T(8,128)(2,1)S(1)}, u32[]{:S(2)}, u32[]{:S(2)}) collective-permute-start(bf16[256,256]{1,0:T(8,128)(2,1)S(1)} %copy.131), channel_id=1, source_target_pairs={{4,0},{8,4},{12,8},{16,12},{20,16},{24,20},{28,24},{0,28},{5,1},{9... | collective-permute-start | bytes 393224 | tf_op jit(solution)/shard_map/while/body/eval_jaxpr/ppermute | solution.py:16
  110.1 4.9 %collective-permute-start.3 = (bf16[256,256]{1,0:T(8,128)(2,1)S(1)}, bf16[256,256]{1,0:T(8,128)(2,1)S(1)}, u32[]{:S(2)}, u32[]{:S(2)}) collective-permute-start(bf16[256,256]{1,0:T(8,128)(2,1)S(1)} %copy.132), channel_id=1, source_target_pairs={{4,0},{8,4},{12,8},{16,12},{20,16},{24,20},{28,24},{0,28},{5,1},{9... | collective-permute-start | bytes 393224 | tf_op jit(solution)/shard_map/while/body/eval_jaxpr/ppermute | solution.py:16
  115.1 8.5 %collective-permute-start = (bf16[256,256]{1,0:T(8,128)(2,1)S(1)}, bf16[256,256]{1,0:T(8,128)(2,1)S(1)}, u32[]{:S(2)}, u32[]{:S(2)}) collective-permute-start(bf16[256,256]{1,0:T(8,128)(2,1)S(1)} %copy.129), channel_id=1, source_target_pairs={{28,0},{0,4},{4,8},{8,12},{12,16},{16,20},{20,24},{24,28},{29,1},{... | collective-permute-start | bytes 393224 | tf_op jit(solution)/shard_map/while/body/eval_jaxpr/ppermute | solution.py:16
  115.9 7.7 %collective-permute-start.1 = (bf16[256,256]{1,0:T(8,128)(2,1)S(1)}, bf16[256,256]{1,0:T(8,128)(2,1)S(1)}, u32[]{:S(2)}, u32[]{:S(2)}) collective-permute-start(bf16[256,256]{1,0:T(8,128)(2,1)S(1)} %copy.130), channel_id=1, source_target_pairs={{28,0},{0,4},{4,8},{8,12},{12,16},{16,20},{20,24},{24,28},{29,1},{... | collective-permute-start | bytes 393224 | tf_op jit(solution)/shard_map/while/body/eval_jaxpr/ppermute | solution.py:16
  116.0 7.6 %collective-permute-start.2 = (bf16[256,256]{1,0:T(8,128)(2,1)S(1)}, bf16[256,256]{1,0:T(8,128)(2,1)S(1)}, u32[]{:S(2)}, u32[]{:S(2)}) collective-permute-start(bf16[256,256]{1,0:T(8,128)(2,1)S(1)} %copy.131), channel_id=1, source_target_pairs={{4,0},{8,4},{12,8},{16,12},{20,16},{24,20},{28,24},{0,28},{5,1},{9... | collective-permute-start | bytes 393224 | tf_op jit(solution)/shard_map/while/body/eval_jaxpr/ppermute | solution.py:16
  118.7 4.9 %collective-permute-start.3 = (bf16[256,256]{1,0:T(8,128)(2,1)S(1)}, bf16[256,256]{1,0:T(8,128)(2,1)S(1)}, u32[]{:S(2)}, u32[]{:S(2)}) collective-permute-start(bf16[256,256]{1,0:T(8,128)(2,1)S(1)} %copy.132), channel_id=1, source_target_pairs={{4,0},{8,4},{12,8},{16,12},{20,16},{24,20},{28,24},{0,28},{5,1},{9... | collective-permute-start | bytes 393224 | tf_op jit(solution)/shard_map/while/body/eval_jaxpr/ppermute | solution.py:16
Sparse Core Ops, SparseCore 0:
  8.9 48.3 all-gather.1
  135.5 41.8 reduce-scatter.1
where the time goes:
time: 186 us
  waiting for transfers between devices  88.7 us (48%)
  matrix products  39.2 us (21%)
  starting transfers between devices  24.9 us (13%)
  other arithmetic  14.2 us (8%)
  between operations  14.2 us (8%)
  local copies, waits for them, and re-layouts  3.76 us (2%)
    all_gather x1, waiting for transfers between devices, shards(): lax.all_gather(text_states, 'head', axis=1, tiled=True)  46.5 us
    reduce_scatter x1, waiting for transfers between devices, shards(): lax.psum_scatter(lax.dot_general(output_weight, attention_output, (((0,),...  41.3 us
    ppermute x28, starting transfers between devices, from_behind(): return lax.ppermute(block, axis, route)  24.9 us
    dot_general x16, matrix products, dense_block(): jnp.einsum('vus,svg->vug', weights.astype(jnp.bfloat16), value_heads, pre...  16.7 us
    dot_general x16, matrix products, dense_block(): jnp.einsum('sxn,lsn->sxl', grouped_queries, key_head_count, preferred_ele...  9.04 us
    reduce_sum x16, other arithmetic, dense_block(): weight_sum = weight_sum * factor + jnp.sum(weights, axis=2)  8.05 us
    dot_general x1, matrix products, shards(): lax.dot_general(output_weight, attention_output, (((0,), (1,)), ((), ()))...  7.11 us
    dot_general x1, matrix products, shards(): jnp.dot(lax.all_gather(text_states, 'head', axis=1, tiled=True), query_we...  6.34 us
  transfers between devices with their start and end apart: 30, of which 2 were waited for; matrix products, arithmetic and copies ran while one was open for 20% of the time, Pallas kernels for 0%

commit v1 on v0

--- a/solution.py
+++ b/solution.py
@@ -32,10 +32,14 @@
     seq_index = lax.axis_index("seq")
     cycle_size = lax.axis_size("seq")
     score_scale = 1.0 / math.sqrt(HD)
+
+    def samples_all_state(w_in):
+        t_next = lax.all_gather(w_in, "head")
+        arr_now = jnp.concatenate(t_next, axis=1)
+        return arr_now
+
     queries = jnp.dot(
-        lax.all_gather(text_states, "head", axis=1, tiled=True),
-        query_weight,
-        preferred_element_type=jnp.float32,
+        samples_all_state(text_states), query_weight, preferred_element_type=jnp.float32
     ).astype(jnp.bfloat16)
     grouped_queries = (
         queries.reshape(text_rows, local_kv, GROUP, HD)

time: 186 us -> 191 us (1.027)
  local copies, waits for them, and re-layouts: 3.76 us -> 7.73 us
    reshape x0 -> x1, local copies, waits for them, and re-layouts: none -> 2.85 us  [samples_all_state(): arr_now = jnp.concatenate(t_next, axis=1)]
  transfers between devices with their start and end apart: 30 -> 30, of which waited for: 2 -> 2; matrix products, arithmetic and copies ran while one was open for 20% -> 19% of each run, Pallas kernels for 0% -> 0%
where the time goes in v1:
time: 191 us; the launch traced here: 190 us
  waiting for transfers between devices  88.5 us (46%)
  matrix products  39.3 us (21%)
  starting transfers between devices  24.9 us (13%)
  between operations  14.3 us (7%)
  other arithmetic  14.2 us (7%)
  local copies, waits for them, and re-layouts  7.73 us (4%)
    all_gather x1, waiting for transfers between devices, samples_all_state(): t_next = lax.all_gather(w_in, 'head')  46.5 us
    reduce_scatter x1, waiting for transfers between devices, shards(): lax.psum_scatter(lax.dot_general(output_weight, attention_output, (((0,),...  41.1 us
    ppermute x28, starting transfers between devices, from_behind(): return lax.ppermute(block, axis, route)  24.9 us
    dot_general x16, matrix products, dense_block(): jnp.einsum('vus,svg->vug', weights.astype(jnp.bfloat16), value_heads, pre...  16.6 us
    dot_general x16, matrix products, dense_block(): jnp.einsum('sxn,lsn->sxl', grouped_queries, key_head_count, preferred_ele...  9.08 us
    reduce_sum x16, other arithmetic, dense_block(): weight_sum = weight_sum * factor + jnp.sum(weights, axis=2)  8.05 us
    dot_general x1, matrix products, shards(): lax.dot_general(output_weight, attention_output, (((0,), (1,)), ((), ()))...  7.11 us
    dot_general x1, matrix products, shards(): jnp.dot(samples_all_state(text_states), query_weight, preferred_element_t...  6.54 us
  transfers between devices with their start and end apart: 30, of which 2 were waited for; matrix products, arithmetic and copies ran while one was open for 19% of the time, Pallas kernels for 0%

profile of v1, /device:TPU:0, one launch (start us, length us, event | category | flops | bytes accessed | tf_op | source)
XLA Modules:
  0.0 190.1 jit_solution(11771245145162486520)
XLA Ops:
  6.5 0.7 all-gather.3.cloned.1.call-update
  7.4 0.7 copy.60
  8.3 0.7 dynamic_slice.3
  9.6 1.1 fusion.71
  10.8 46.5 %all-gather.3.cloned.1.call-done = bf16[1024,1024]{1,0:T(8,128)(2,1)} async-done(((bf16[256,1024]{1,0:T(8,128)(2,1)}), bf16[1024,1024]{1,0:T(8,128)(2,1)}) %all-gather.3.cloned.1.call-update) | async-done | bytes 2097168 | tf_op jit(solution)/shard_map/all_gather | solution.py:37
  57.3 2.8 %copy.61 = bf16[256,4,1024]{0,2,1:T(8,128)(2,1)S(1)} copy(bf16[256,4,1024]{2,0,1:T(8,128)(2,1)} %bitcast.121) | data formatting | bytes 4194304 | tf_op jit(solution)/shard_map/reshape | solution.py:38
  60.2 6.5 %convolution_convert_fusion.1 = bf16[256,1024]{1,0:T(8,128)(2,1)} fusion(bf16[256,4096]{0,1:T(8,128)(2,1)S(1)} %bitcast.119, bf16[4096,1024]{1,0:T(8,128)(2,1)} %param.11), kind=kOutput, calls=%fused_computation.65 | convolution fusion | flops 2147745792 | bytes 11010048 | tf_op jit(solution)/shard_map/dot_general | solution.py:41
  66.7 1.5 reshape.269
  68.3 59.5 %while.28 = (s32[]{:T(128)}, f32[2,1024]{1,0:T(2,128)S(1)}, f32[2,1024]{1,0:T(2,128)S(1)}, f32[2,1024,128]{2,1,0:T(8,128)S(1)}, bf16[256,256]{1,0:T(8,128)(2,1)S...) while((s32[]{:T(128)}, f32[2,1024]{1,0:T(2,128)S(1)}, ...), condition=%wide.region_8.9_spmd.clone, body=%wide.region_1.8_spmd.clone.sunk | while | flops 550279168 | bytes 23832240 | solution.py:112
  68.4 1.6 collective-permute-start.1
  70.0 1.1 collective-permute-start.2
  71.2 0.5 collective-permute-start.3
  72.2 0.6 select_reduce_fusion.6
  72.8 0.6 select_reduce_fusion.7
  73.4 0.5 fusion.116
  74.4 1.2 fusion.118
  75.7 0.8 convolution_add_fusion.5
  76.6 1.2 collective-permute-start
  77.9 2.7 %collective-permute-start.2 = (bf16[256,256]{1,0:T(8,128)(2,1)S(1)}, bf16[256,256]{1,0:T(8,128)(2,1)S(1)}, u32[]{:S(2)}, u32[]{:S(2)}) collective-permute-start(bf16[256,256]{1,0:T(8,128)(2,1)S(1)} %copy.148), channel_id=1, source_target_pairs={{4,0},{8,4},{12,8},{16,12},{20,16},{24,20},{28,24},{0,28},{5,1},{9... | collective-permute-start | bytes 393224 | tf_op jit(solution)/shard_map/while/body/eval_jaxpr/ppermute | solution.py:16
  81.2 0.6 select_reduce_fusion.6
  81.7 0.6 select_reduce_fusion.7
  82.3 0.5 fusion.116
  83.4 1.2 fusion.118
  84.6 0.8 convolution_add_fusion.5
  85.5 0.8 collective-permute-start
  86.5 2.7 %collective-permute-start.2 = (bf16[256,256]{1,0:T(8,128)(2,1)S(1)}, bf16[256,256]{1,0:T(8,128)(2,1)S(1)}, u32[]{:S(2)}, u32[]{:S(2)}) collective-permute-start(bf16[256,256]{1,0:T(8,128)(2,1)S(1)} %copy.148), channel_id=1, source_target_pairs={{4,0},{8,4},{12,8},{16,12},{20,16},{24,20},{28,24},{0,28},{5,1},{9... | collective-permute-start | bytes 393224 | tf_op jit(solution)/shard_map/while/body/eval_jaxpr/ppermute | solution.py:16
  89.7 0.6 select_reduce_fusion.6
  90.3 0.6 select_reduce_fusion.7
  90.9 0.5 fusion.116
  92.0 1.2 fusion.118
  93.2 0.8 convolution_add_fusion.5
  94.7 2.7 %collective-permute-start.2 = (bf16[256,256]{1,0:T(8,128)(2,1)S(1)}, bf16[256,256]{1,0:T(8,128)(2,1)S(1)}, u32[]{:S(2)}, u32[]{:S(2)}) collective-permute-start(bf16[256,256]{1,0:T(8,128)(2,1)S(1)} %copy.148), channel_id=1, source_target_pairs={{4,0},{8,4},{12,8},{16,12},{20,16},{24,20},{28,24},{0,28},{5,1},{9... | collective-permute-start | bytes 393224 | tf_op jit(solution)/shard_map/while/body/eval_jaxpr/ppermute | solution.py:16
  98.0 0.6 select_reduce_fusion.6
  98.6 0.6 select_reduce_fusion.7
  99.2 0.5 fusion.116
  100.2 1.2 fusion.118
  101.4 0.8 convolution_add_fusion.5
  103.0 2.7 %collective-permute-start.2 = (bf16[256,256]{1,0:T(8,128)(2,1)S(1)}, bf16[256,256]{1,0:T(8,128)(2,1)S(1)}, u32[]{:S(2)}, u32[]{:S(2)}) collective-permute-start(bf16[256,256]{1,0:T(8,128)(2,1)S(1)} %copy.148), channel_id=1, source_target_pairs={{4,0},{8,4},{12,8},{16,12},{20,16},{24,20},{28,24},{0,28},{5,1},{9... | collective-permute-start | bytes 393224 | tf_op jit(solution)/shard_map/while/body/eval_jaxpr/ppermute | solution.py:16
  106.2 0.6 select_reduce_fusion.6
  106.8 0.6 select_reduce_fusion.7
  107.4 0.5 fusion.116
  108.5 1.2 fusion.118
  109.7 0.8 convolution_add_fusion.5
  110.6 0.7 collective-permute-start
  111.4 2.7 %collective-permute-start.2 = (bf16[256,256]{1,0:T(8,128)(2,1)S(1)}, bf16[256,256]{1,0:T(8,128)(2,1)S(1)}, u32[]{:S(2)}, u32[]{:S(2)}) collective-permute-start(bf16[256,256]{1,0:T(8,128)(2,1)S(1)} %copy.148), channel_id=1, source_target_pairs={{4,0},{8,4},{12,8},{16,12},{20,16},{24,20},{28,24},{0,28},{5,1},{9... | collective-permute-start | bytes 393224 | tf_op jit(solution)/shard_map/while/body/eval_jaxpr/ppermute | solution.py:16
  114.7 0.6 select_reduce_fusion.6
  115.3 0.6 select_reduce_fusion.7
  115.9 0.5 fusion.116
  116.9 1.2 fusion.118
  118.1 0.8 convolution_add_fusion.5
  119.1 0.8 collective-permute-start
  120.0 2.7 %collective-permute-start.2 = (bf16[256,256]{1,0:T(8,128)(2,1)S(1)}, bf16[256,256]{1,0:T(8,128)(2,1)S(1)}, u32[]{:S(2)}, u32[]{:S(2)}) collective-permute-start(bf16[256,256]{1,0:T(8,128)(2,1)S(1)} %copy.148), channel_id=1, source_target_pairs={{4,0},{8,4},{12,8},{16,12},{20,16},{24,20},{28,24},{0,28},{5,1},{9... | collective-permute-start | bytes 393224 | tf_op jit(solution)/shard_map/while/body/eval_jaxpr/ppermute | solution.py:16
  123.3 0.6 select_reduce_fusion.6
  123.8 0.6 select_reduce_fusion.7
  124.4 0.5 fusion.116
  125.5 1.2 fusion.118
  126.7 0.8 convolution_add_fusion.5
  127.8 0.6 select_reduce_fusion.2
  128.4 0.6 select_reduce_fusion.3
  130.0 1.2 fusion.41
  131.2 1.0 fusion.42
  132.4 7.1 %fusion.35 = bf16[4096,256]{0,1:T(8,128)(2,1)} fusion(bf16[256,1024]{0,1:T(8,128)(2,1)S(1)} %bitcast.120, bf16[1024,4096]{1,0:T(8,128)(2,1)} %param.14), kind=kOutput, calls=%fused_computation.51 | convolution fusion | flops 2148532224 | bytes 11010048 | tf_op jit(solution)/shard_map/dot_general | solution.py:127
  140.3 41.1 %reduce-scatter.2.cloned.1.call-done = bf16[1024,256]{0,1:T(8,128)(2,1)} async-done(((bf16[4096,256]{0,1:T(8,128)(2,1)}), bf16[1024,256]{0,1:T(8,128)(2,1)}) %reduce-scatter.2.cloned.1.call-update) | async-done | bytes 524304 | tf_op jit(solution)/shard_map/reduce_scatter | solution.py:126
  181.4 1.9 %fusion.53 = bf16[256,1024]{1,0:T(8,128)(2,1)} fusion(bf16[1024,256]{0,1:T(8,128)(2,1)} %reduce-scatter.2.cloned.1.call-done, f32[]{:T(128)} %bitcast), kind=kLoop, calls=%fused_computation.75 | loop fusion | flops 786432 | bytes 1048580 | tf_op jit(solution)/shard_map/convert_element_type | solution.py:137
  (157 shorter events, 11.6 us)
Async XLA Ops:
  6.5 50.8 %all-gather.3.cloned.1.call-start = ((), (), s32[]{:S(2)}) async-start(), calls=%async_computation.2 | async-start | bytes 2621440 | tf_op jit(solution)/shard_map/all_gather | solution.py:37
  7.3 174.1 %reduce-scatter.2.cloned.1.call-start = ((), (), s32[]{:S(2)}) async-start(), calls=%async_computation.1 | async-start | bytes 2621440 | tf_op jit(solution)/shard_map/reduce_scatter | solution.py:126
  66.7 1.6 copy-start
  68.3 8.2 %collective-permute-start = (bf16[256,256]{1,0:T(8,128)(2,1)S(1)}, bf16[256,256]{1,0:T(8,128)(2,1)S(1)}, u32[]{:S(2)}, u32[]{:S(2)}) collective-permute-start(bf16[256,256]{1,0:T(8,128)(2,1)S(1)} %copy.146), channel_id=1, source_target_pairs={{28,0},{0,4},{4,8},{8,12},{12,16},{16,20},{20,24},{24,28},{29,1},{... | collective-permute-start | bytes 393224 | tf_op jit(solution)/shard_map/while/body/eval_jaxpr/ppermute | solution.py:16
  68.4 8.1 %collective-permute-start.1 = (bf16[256,256]{1,0:T(8,128)(2,1)S(1)}, bf16[256,256]{1,0:T(8,128)(2,1)S(1)}, u32[]{:S(2)}, u32[]{:S(2)}) collective-permute-start(bf16[256,256]{1,0:T(8,128)(2,1)S(1)} %copy.147), channel_id=1, source_target_pairs={{28,0},{0,4},{4,8},{8,12},{12,16},{16,20},{20,24},{24,28},{29,1},{... | collective-permute-start | bytes 393224 | tf_op jit(solution)/shard_map/while/body/eval_jaxpr/ppermute | solution.py:16
  70.0 6.5 %collective-permute-start.2 = (bf16[256,256]{1,0:T(8,128)(2,1)S(1)}, bf16[256,256]{1,0:T(8,128)(2,1)S(1)}, u32[]{:S(2)}, u32[]{:S(2)}) collective-permute-start(bf16[256,256]{1,0:T(8,128)(2,1)S(1)} %copy.148), channel_id=1, source_target_pairs={{4,0},{8,4},{12,8},{16,12},{20,16},{24,20},{28,24},{0,28},{5,1},{9... | collective-permute-start | bytes 393224 | tf_op jit(solution)/shard_map/while/body/eval_jaxpr/ppermute | solution.py:16
  71.2 5.3 %collective-permute-start.3 = (bf16[256,256]{1,0:T(8,128)(2,1)S(1)}, bf16[256,256]{1,0:T(8,128)(2,1)S(1)}, u32[]{:S(2)}, u32[]{:S(2)}) collective-permute-start(bf16[256,256]{1,0:T(8,128)(2,1)S(1)} %copy.149), channel_id=1, source_target_pairs={{4,0},{8,4},{12,8},{16,12},{20,16},{24,20},{28,24},{0,28},{5,1},{9... | collective-permute-start | bytes 393224 | tf_op jit(solution)/shard_map/while/body/eval_jaxpr/ppermute | solution.py:16
  76.6 8.9 %collective-permute-start = (bf16[256,256]{1,0:T(8,128)(2,1)S(1)}, bf16[256,256]{1,0:T(8,128)(2,1)S(1)}, u32[]{:S(2)}, u32[]{:S(2)}) collective-permute-start(bf16[256,256]{1,0:T(8,128)(2,1)S(1)} %copy.146), channel_id=1, source_target_pairs={{28,0},{0,4},{4,8},{8,12},{12,16},{16,20},{20,24},{24,28},{29,1},{... | collective-permute-start | bytes 393224 | tf_op jit(solution)/shard_map/while/body/eval_jaxpr/ppermute | solution.py:16
  77.8 7.7 %collective-permute-start.1 = (bf16[256,256]{1,0:T(8,128)(2,1)S(1)}, bf16[256,256]{1,0:T(8,128)(2,1)S(1)}, u32[]{:S(2)}, u32[]{:S(2)}) collective-permute-start(bf16[256,256]{1,0:T(8,128)(2,1)S(1)} %copy.147), channel_id=1, source_target_pairs={{28,0},{0,4},{4,8},{8,12},{12,16},{16,20},{20,24},{24,28},{29,1},{... | collective-permute-start | bytes 393224 | tf_op jit(solution)/shard_map/while/body/eval_jaxpr/ppermute | solution.py:16
  77.9 7.6 %collective-permute-start.2 = (bf16[256,256]{1,0:T(8,128)(2,1)S(1)}, bf16[256,256]{1,0:T(8,128)(2,1)S(1)}, u32[]{:S(2)}, u32[]{:S(2)}) collective-permute-start(bf16[256,256]{1,0:T(8,128)(2,1)S(1)} %copy.148), channel_id=1, source_target_pairs={{4,0},{8,4},{12,8},{16,12},{20,16},{24,20},{28,24},{0,28},{5,1},{9... | collective-permute-start | bytes 393224 | tf_op jit(solution)/shard_map/while/body/eval_jaxpr/ppermute | solution.py:16
  80.6 4.9 %collective-permute-start.3 = (bf16[256,256]{1,0:T(8,128)(2,1)S(1)}, bf16[256,256]{1,0:T(8,128)(2,1)S(1)}, u32[]{:S(2)}, u32[]{:S(2)}) collective-permute-start(bf16[256,256]{1,0:T(8,128)(2,1)S(1)} %copy.149), channel_id=1, source_target_pairs={{4,0},{8,4},{12,8},{16,12},{20,16},{24,20},{28,24},{0,28},{5,1},{9... | collective-permute-start | bytes 393224 | tf_op jit(solution)/shard_map/while/body/eval_jaxpr/ppermute | solution.py:16
  85.5 8.5 %collective-permute-start = (bf16[256,256]{1,0:T(8,128)(2,1)S(1)}, bf16[256,256]{1,0:T(8,128)(2,1)S(1)}, u32[]{:S(2)}, u32[]{:S(2)}) collective-permute-start(bf16[256,256]{1,0:T(8,128)(2,1)S(1)} %copy.146), channel_id=1, source_target_pairs={{28,0},{0,4},{4,8},{8,12},{12,16},{16,20},{20,24},{24,28},{29,1},{... | collective-permute-start | bytes 393224 | tf_op jit(solution)/shard_map/while/body/eval_jaxpr/ppermute | solution.py:16
  86.4 7.7 %collective-permute-start.1 = (bf16[256,256]{1,0:T(8,128)(2,1)S(1)}, bf16[256,256]{1,0:T(8,128)(2,1)S(1)}, u32[]{:S(2)}, u32[]{:S(2)}) collective-permute-start(bf16[256,256]{1,0:T(8,128)(2,1)S(1)} %copy.147), channel_id=1, source_target_pairs={{28,0},{0,4},{4,8},{8,12},{12,16},{16,20},{20,24},{24,28},{29,1},{... | collective-permute-start | bytes 393224 | tf_op jit(solution)/shard_map/while/body/eval_jaxpr/ppermute | solution.py:16
  86.5 7.6 %collective-permute-start.2 = (bf16[256,256]{1,0:T(8,128)(2,1)S(1)}, bf16[256,256]{1,0:T(8,128)(2,1)S(1)}, u32[]{:S(2)}, u32[]{:S(2)}) collective-permute-start(bf16[256,256]{1,0:T(8,128)(2,1)S(1)} %copy.148), channel_id=1, source_target_pairs={{4,0},{8,4},{12,8},{16,12},{20,16},{24,20},{28,24},{0,28},{5,1},{9... | collective-permute-start | bytes 393224 | tf_op jit(solution)/shard_map/while/body/eval_jaxpr/ppermute | solution.py:16
  89.1 4.9 %collective-permute-start.3 = (bf16[256,256]{1,0:T(8,128)(2,1)S(1)}, bf16[256,256]{1,0:T(8,128)(2,1)S(1)}, u32[]{:S(2)}, u32[]{:S(2)}) collective-permute-start(bf16[256,256]{1,0:T(8,128)(2,1)S(1)} %copy.149), channel_id=1, source_target_pairs={{4,0},{8,4},{12,8},{16,12},{20,16},{24,20},{28,24},{0,28},{5,1},{9... | collective-permute-start | bytes 393224 | tf_op jit(solution)/shard_map/while/body/eval_jaxpr/ppermute | solution.py:16
  94.1 8.2 %collective-permute-start = (bf16[256,256]{1,0:T(8,128)(2,1)S(1)}, bf16[256,256]{1,0:T(8,128)(2,1)S(1)}, u32[]{:S(2)}, u32[]{:S(2)}) collective-permute-start(bf16[256,256]{1,0:T(8,128)(2,1)S(1)} %copy.146), channel_id=1, source_target_pairs={{28,0},{0,4},{4,8},{8,12},{12,16},{16,20},{20,24},{24,28},{29,1},{... | collective-permute-start | bytes 393224 | tf_op jit(solution)/shard_map/while/body/eval_jaxpr/ppermute | solution.py:16
  94.6 7.7 %collective-permute-start.1 = (bf16[256,256]{1,0:T(8,128)(2,1)S(1)}, bf16[256,256]{1,0:T(8,128)(2,1)S(1)}, u32[]{:S(2)}, u32[]{:S(2)}) collective-permute-start(bf16[256,256]{1,0:T(8,128)(2,1)S(1)} %copy.147), channel_id=1, source_target_pairs={{28,0},{0,4},{4,8},{8,12},{12,16},{16,20},{20,24},{24,28},{29,1},{... | collective-permute-start | bytes 393224 | tf_op jit(solution)/shard_map/while/body/eval_jaxpr/ppermute | solution.py:16
  94.7 7.6 %collective-permute-start.2 = (bf16[256,256]{1,0:T(8,128)(2,1)S(1)}, bf16[256,256]{1,0:T(8,128)(2,1)S(1)}, u32[]{:S(2)}, u32[]{:S(2)}) collective-permute-start(bf16[256,256]{1,0:T(8,128)(2,1)S(1)} %copy.148), channel_id=1, source_target_pairs={{4,0},{8,4},{12,8},{16,12},{20,16},{24,20},{28,24},{0,28},{5,1},{9... | collective-permute-start | bytes 393224 | tf_op jit(solution)/shard_map/while/body/eval_jaxpr/ppermute | solution.py:16
  97.4 4.9 %collective-permute-start.3 = (bf16[256,256]{1,0:T(8,128)(2,1)S(1)}, bf16[256,256]{1,0:T(8,128)(2,1)S(1)}, u32[]{:S(2)}, u32[]{:S(2)}) collective-permute-start(bf16[256,256]{1,0:T(8,128)(2,1)S(1)} %copy.149), channel_id=1, source_target_pairs={{4,0},{8,4},{12,8},{16,12},{20,16},{24,20},{28,24},{0,28},{5,1},{9... | collective-permute-start | bytes 393224 | tf_op jit(solution)/shard_map/while/body/eval_jaxpr/ppermute | solution.py:16
  102.4 8.2 %collective-permute-start = (bf16[256,256]{1,0:T(8,128)(2,1)S(1)}, bf16[256,256]{1,0:T(8,128)(2,1)S(1)}, u32[]{:S(2)}, u32[]{:S(2)}) collective-permute-start(bf16[256,256]{1,0:T(8,128)(2,1)S(1)} %copy.146), channel_id=1, source_target_pairs={{28,0},{0,4},{4,8},{8,12},{12,16},{16,20},{20,24},{24,28},{29,1},{... | collective-permute-start | bytes 393224 | tf_op jit(solution)/shard_map/while/body/eval_jaxpr/ppermute | solution.py:16
  102.9 7.7 %collective-permute-start.1 = (bf16[256,256]{1,0:T(8,128)(2,1)S(1)}, bf16[256,256]{1,0:T(8,128)(2,1)S(1)}, u32[]{:S(2)}, u32[]{:S(2)}) collective-permute-start(bf16[256,256]{1,0:T(8,128)(2,1)S(1)} %copy.147), channel_id=1, source_target_pairs={{28,0},{0,4},{4,8},{8,12},{12,16},{16,20},{20,24},{24,28},{29,1},{... | collective-permute-start | bytes 393224 | tf_op jit(solution)/shard_map/while/body/eval_jaxpr/ppermute | solution.py:16
  103.0 7.6 %collective-permute-start.2 = (bf16[256,256]{1,0:T(8,128)(2,1)S(1)}, bf16[256,256]{1,0:T(8,128)(2,1)S(1)}, u32[]{:S(2)}, u32[]{:S(2)}) collective-permute-start(bf16[256,256]{1,0:T(8,128)(2,1)S(1)} %copy.148), channel_id=1, source_target_pairs={{4,0},{8,4},{12,8},{16,12},{20,16},{24,20},{28,24},{0,28},{5,1},{9... | collective-permute-start | bytes 393224 | tf_op jit(solution)/shard_map/while/body/eval_jaxpr/ppermute | solution.py:16
  105.6 4.9 %collective-permute-start.3 = (bf16[256,256]{1,0:T(8,128)(2,1)S(1)}, bf16[256,256]{1,0:T(8,128)(2,1)S(1)}, u32[]{:S(2)}, u32[]{:S(2)}) collective-permute-start(bf16[256,256]{1,0:T(8,128)(2,1)S(1)} %copy.149), channel_id=1, source_target_pairs={{4,0},{8,4},{12,8},{16,12},{20,16},{24,20},{28,24},{0,28},{5,1},{9... | collective-permute-start | bytes 393224 | tf_op jit(solution)/shard_map/while/body/eval_jaxpr/ppermute | solution.py:16
  110.6 8.4 %collective-permute-start = (bf16[256,256]{1,0:T(8,128)(2,1)S(1)}, bf16[256,256]{1,0:T(8,128)(2,1)S(1)}, u32[]{:S(2)}, u32[]{:S(2)}) collective-permute-start(bf16[256,256]{1,0:T(8,128)(2,1)S(1)} %copy.146), channel_id=1, source_target_pairs={{28,0},{0,4},{4,8},{8,12},{12,16},{16,20},{20,24},{24,28},{29,1},{... | collective-permute-start | bytes 393224 | tf_op jit(solution)/shard_map/while/body/eval_jaxpr/ppermute | solution.py:16
  111.3 7.7 %collective-permute-start.1 = (bf16[256,256]{1,0:T(8,128)(2,1)S(1)}, bf16[256,256]{1,0:T(8,128)(2,1)S(1)}, u32[]{:S(2)}, u32[]{:S(2)}) collective-permute-start(bf16[256,256]{1,0:T(8,128)(2,1)S(1)} %copy.147), channel_id=1, source_target_pairs={{28,0},{0,4},{4,8},{8,12},{12,16},{16,20},{20,24},{24,28},{29,1},{... | collective-permute-start | bytes 393224 | tf_op jit(solution)/shard_map/while/body/eval_jaxpr/ppermute | solution.py:16
  111.4 7.6 %collective-permute-start.2 = (bf16[256,256]{1,0:T(8,128)(2,1)S(1)}, bf16[256,256]{1,0:T(8,128)(2,1)S(1)}, u32[]{:S(2)}, u32[]{:S(2)}) collective-permute-start(bf16[256,256]{1,0:T(8,128)(2,1)S(1)} %copy.148), channel_id=1, source_target_pairs={{4,0},{8,4},{12,8},{16,12},{20,16},{24,20},{28,24},{0,28},{5,1},{9... | collective-permute-start | bytes 393224 | tf_op jit(solution)/shard_map/while/body/eval_jaxpr/ppermute | solution.py:16
  114.1 4.9 %collective-permute-start.3 = (bf16[256,256]{1,0:T(8,128)(2,1)S(1)}, bf16[256,256]{1,0:T(8,128)(2,1)S(1)}, u32[]{:S(2)}, u32[]{:S(2)}) collective-permute-start(bf16[256,256]{1,0:T(8,128)(2,1)S(1)} %copy.149), channel_id=1, source_target_pairs={{4,0},{8,4},{12,8},{16,12},{20,16},{24,20},{28,24},{0,28},{5,1},{9... | collective-permute-start | bytes 393224 | tf_op jit(solution)/shard_map/while/body/eval_jaxpr/ppermute | solution.py:16
  119.1 8.5 %collective-permute-start = (bf16[256,256]{1,0:T(8,128)(2,1)S(1)}, bf16[256,256]{1,0:T(8,128)(2,1)S(1)}, u32[]{:S(2)}, u32[]{:S(2)}) collective-permute-start(bf16[256,256]{1,0:T(8,128)(2,1)S(1)} %copy.146), channel_id=1, source_target_pairs={{28,0},{0,4},{4,8},{8,12},{12,16},{16,20},{20,24},{24,28},{29,1},{... | collective-permute-start | bytes 393224 | tf_op jit(solution)/shard_map/while/body/eval_jaxpr/ppermute | solution.py:16
  119.9 7.7 %collective-permute-start.1 = (bf16[256,256]{1,0:T(8,128)(2,1)S(1)}, bf16[256,256]{1,0:T(8,128)(2,1)S(1)}, u32[]{:S(2)}, u32[]{:S(2)}) collective-permute-start(bf16[256,256]{1,0:T(8,128)(2,1)S(1)} %copy.147), channel_id=1, source_target_pairs={{28,0},{0,4},{4,8},{8,12},{12,16},{16,20},{20,24},{24,28},{29,1},{... | collective-permute-start | bytes 393224 | tf_op jit(solution)/shard_map/while/body/eval_jaxpr/ppermute | solution.py:16
  120.0 7.6 %collective-permute-start.2 = (bf16[256,256]{1,0:T(8,128)(2,1)S(1)}, bf16[256,256]{1,0:T(8,128)(2,1)S(1)}, u32[]{:S(2)}, u32[]{:S(2)}) collective-permute-start(bf16[256,256]{1,0:T(8,128)(2,1)S(1)} %copy.148), channel_id=1, source_target_pairs={{4,0},{8,4},{12,8},{16,12},{20,16},{24,20},{28,24},{0,28},{5,1},{9... | collective-permute-start | bytes 393224 | tf_op jit(solution)/shard_map/while/body/eval_jaxpr/ppermute | solution.py:16
  122.7 4.9 %collective-permute-start.3 = (bf16[256,256]{1,0:T(8,128)(2,1)S(1)}, bf16[256,256]{1,0:T(8,128)(2,1)S(1)}, u32[]{:S(2)}, u32[]{:S(2)}) collective-permute-start(bf16[256,256]{1,0:T(8,128)(2,1)S(1)} %copy.149), channel_id=1, source_target_pairs={{4,0},{8,4},{12,8},{16,12},{20,16},{24,20},{28,24},{0,28},{5,1},{9... | collective-permute-start | bytes 393224 | tf_op jit(solution)/shard_map/while/body/eval_jaxpr/ppermute | solution.py:16
Sparse Core Ops, SparseCore 0:
  8.9 48.3 all-gather.2
  139.7 41.6 reduce-scatter.1
